TPU v7x, 32 devices: a whole 2x2x4 slice. The times are simulated.
32 devices in a mesh: leaf: 8 (over y, x, core), rows: 4 (over z).
Axes of the slice: x: 2, y: 2, z: 4, core: 2. Of those that a mesh axis runs over, the one named last changes fastest.
Arguments:
- right_side: float32 [8, 2, 64, 512], P('leaf', None, None, 'rows'), as said below
- diag_inverse: float32 [8, 2, 512, 128], P('leaf', None, 'rows'), as said below
- sep_lower: float32 [8, 2, 512, 512], P('leaf', None, 'rows'), as said below
- front_lower: float32 [8, 2, 1024, 512], P('leaf', None, None, 'rows'), as said below
- front_index: int32 [8, 2, 1024], P('leaf'), may hold values from 0 to 1535, as said below
Outputs:
- solution: float32 [8, 2, 64, 512], P('leaf', None, None, 'rows')
- top_update: float32 [8, 2, 64, 512], P('leaf', None, None, 'rows')
Inputs may be any that keep to these rules, and one draw needn't show every extreme that they name: `front_index`: for each leaf index and slot s the 1024 entries are distinct, lie below (3 - s) * 512, and are the same on all 2**s leaf indices of the slot's subtree. `right_side`: entries of slot s are the same on all 2**s leaf indices of the slot's subtree. `diag_inverse`: entries of slot s are the same on all 2**s leaf indices of the slot's subtree. `sep_lower`: entries of slot s are the same on all 2**s leaf indices of the slot's subtree. `front_lower`: entries of slot s are the same on all 2**s leaf indices of the slot's subtree.
All inputs are finite; a program needn't handle non-finite values.
Results may differ from a plain program's by a relative error of at most 0.00011.
Values sent between devices are 32-bit elements; how exact they have to be, the bound alone decides.
A program may use at most 128 MiB of HBM per device.

v0:
```python
import jax
import jax.numpy as jnp
from jax import lax
from jax.sharding import PartitionSpec as P

exact_precision = lax.Precision.HIGHEST


def partner(value, axis, apart):
    mask = 2**apart
    pairs = [(source, source ^ mask) for source in range(lax.axis_size(axis))]
    return lax.ppermute(value, axis, pairs)


def product(left, right):
    return lax.dot_general(
        left,
        right,
        (((left.ndim - 1,), (right.ndim - 1,)), ((), ())),
        precision=exact_precision,
        preferred_element_type=jnp.float32,
    )


def solve_rows(target, inverse, prefixes, width):
    solved = []
    for block, prefix in enumerate(prefixes):
        first = block * width
        total = target[:, first : first + width]
        if block > 0:
            total = total - product(jnp.concatenate(solved, axis=1), prefix)
        solved.append(product(total, inverse[first : first + width]))
    return jnp.concatenate(solved, axis=1)


def on_device(right_side, diag_inverse, sep_lower, front_lower, front_index):
    levels = right_side.shape[1]
    vectors = right_side.shape[2]
    width = right_side.shape[3]
    blocks = lax.axis_size("rows")
    here = lax.axis_index("rows")
    depth = levels + 1
    targets = right_side[0]
    inverses = diag_inverse[0]
    lowers = sep_lower[0]
    fronts = front_lower[0]
    indices = front_index[0]
    lower_all, inverse_all = (
        lax.all_gather(lowers, "rows", axis=1, tiled=True),
        lax.all_gather(inverses, "rows", axis=1, tiled=True),
    )
    prefix_rows = [
        lower_all[:, block * width : (block + 1) * width, : block * width]
        for block in range(blocks)
    ]
    pending = None
    solutions = []
    for level in range(levels):
        height = depth - level
        if level == 0:
            target = targets[0]
        else:
            pending = pending + partner(pending, "leaf", level - 1)
            target = targets[level] - pending[:, height * width :]
            pending = pending[:, : height * width]
        gathered = lax.all_gather(target, "rows", axis=1, tiled=True)
        joined = solve_rows(
            gathered, inverse_all[level], [rows[level] for rows in prefix_rows], width
        )
        own_block = lax.dynamic_slice_in_dim(joined, here * width, width, 1)
        solutions.append(own_block)
        partial_front = product(own_block, fronts[level])
        summed = lax.psum(partial_front, "rows")
        positions = jnp.arange(height * width, dtype=jnp.int32)
        wanted = positions // width * (blocks * width) + here * width + positions % width
        hits = (wanted[:, None] == indices[level][None, :]).astype(jnp.float32)
        update = product(summed, hits)
        pending = update if level == 0 else pending + update
    top = pending.reshape(vectors, 2, width).transpose(1, 0, 2)
    return (jnp.stack(solutions, axis=0)[None], top[None])


def solution(mesh):
    in_specs = (
        P("leaf", None, None, "rows"),
        P("leaf", None, "rows", None),
        P("leaf", None, "rows", None),
        P("leaf", None, None, "rows"),
        P("leaf", None, None),
    )
    out_specs = (P("leaf", None, None, "rows"), P("leaf", None, None, "rows"))
    return jax.shard_map(
        on_device, mesh=mesh, in_specs=in_specs, out_specs=out_specs, check_vma=False
    )
```

profile of v0, /device:TPU:0, one launch (start us, length us, event | category | flops | bytes accessed | tf_op | source)
XLA Modules:
  0.0 174.2 jit_solution(17245503545314237015)
XLA Ops:
  7.2 0.7 all-gather.5.cloned.1.call-update
  8.0 0.8 slice.139
  8.7 15.2 %all-gather = f32[1,1,64,512]{3,2,1,0:T(8,128)S(1)} all-gather(f32[1,1,64,128]{3,2,1,0:T(8,128)S(1)} %slice.139), channel_id=2, replica_groups=mesh['leaf'=8,'rows'=4] {'rows'}, dimensions={3}, use_global_device_ids=true | all-gather | bytes 163840 | tf_op jit(solution)/shard_map/all_gather | solution.py:66
  24.0 23.7 %all-gather.1 = f32[1,2,512,128]{3,2,1,0:T(8,128)S(1)} all-gather(f32[1,2,128,128]{3,2,1,0:T(8,128)} %param.6), channel_id=3, replica_groups=mesh['leaf'=8,'rows'=4] {'rows'}, dimensions={2}, use_global_device_ids=true | all-gather | bytes 655360 | tf_op jit(solution)/shard_map/all_gather | solution.py:50
  47.9 18.6 %all-gather.5.cloned.1.call-done = f32[1,2,512,512]{3,2,1,0:T(8,128)} async-done(((f32[1,2,128,512]{3,2,1,0:T(8,128)}), f32[1,2,512,512]{3,2,1,0:T(8,128)}) %all-gather.5.cloned.1.call-update) | async-done | bytes 2097168 | tf_op jit(solution)/shard_map/all_gather | solution.py:49
  66.5 1.1 convolution_subtract_fusion.2
  67.9 1.2 convolution_subtract_fusion.1
  69.0 0.2 fusion.33
  69.3 1.3 convolution_subtract_fusion
  70.9 1.4 fusion.8
  72.4 34.6 %all-reduce.3.cloned.1.call-done = f32[64,1024]{1,0:T(8,128)} async-done(((f32[64,1024]{1,0:T(8,128)}), f32[64,1024]{1,0:T(8,128)}) %all-reduce.3.cloned.1.call-update) | async-done | bytes 262160 | tf_op jit(solution)/shard_map/psum | solution.py:73
  107.0 1.9 %fusion = f32[64,384]{1,0:T(8,128)S(1)} fusion(f32[64,1024]{1,0:T(8,128)} %all-reduce.3.cloned.1.call-done, s32[1024]{0:T(1024)S(1)} %bitcast.100, s32[384]{0:T(512)S(1)} %fusion.56), kind=kOutput, calls=%fused_computation | convolution fusion | flops 302383104 | bytes 366080 | tf_op jit(solution)/shard_map/dot_general | solution.py:16
  109.0 1.3 collective-permute-done
  110.3 13.3 %all_gather.15 = f32[64,512]{1,0:T(8,128)S(1)} all-gather(f32[64,128]{1,0:T(8,128)S(1)} %slice_subtract_fusion.6), channel_id=1, replica_groups=mesh['leaf'=8,'rows'=4] {'rows'}, dimensions={1}, use_global_device_ids=true | all-gather | bytes 163840 | tf_op jit(solution)/shard_map/all_gather | solution.py:66
  123.9 1.1 fusion.30
  125.0 0.2 fusion.29
  125.3 1.2 fusion.15
  126.4 0.2 fusion.28
  126.7 1.3 fusion.14
  128.3 1.4 fusion.6
  129.7 0.6 maximum_bitcast_fusion
  130.3 35.0 %all-reduce.5.cloned.1.call-done = f32[64,1024]{1,0:T(8,128)} async-done(((f32[64,1024]{1,0:T(8,128)}), f32[64,1024]{1,0:T(8,128)}) %all-reduce.5.cloned.1.call-update) | async-done | bytes 262160 | tf_op jit(solution)/shard_map/psum | solution.py:73
  165.3 1.6 fusion.26
  167.0 0.6 copy.10
  (24 shorter events, 1.5 us)
Async XLA Ops:
  7.2 63.7 %copy-start = (f32[1,2,1024,128]{3,2,1,0:T(8,128)S(1)}, f32[1,2,1024,128]{3,2,1,0:T(8,128)}, u32[]{:S(2)}) copy-start(f32[1,2,1024,128]{3,2,1,0:T(8,128)} %param.8) | copy-start | bytes 3145732
  7.2 65.2 %copy-start.2 = (s32[1,2,1024]{2,1,0:T(2,128)S(1)}, s32[1,2,1024]{2,1,0:T(2,128)}, u32[]{:S(2)}) copy-start(s32[1,2,1024]{2,1,0:T(2,128)} %param.9) | copy-start | bytes 24580
  7.2 59.4 %all-gather.5.cloned.1.call-start = ((), (), s32[]{:S(2)}) async-start(), calls=%async_computation.2 | async-start | bytes 2621440 | tf_op jit(solution)/shard_map/all_gather | solution.py:49
  7.9 99.1 %all-reduce.3.cloned.1.call-start = ((), (), s32[]{:S(2)}) async-start(), calls=%async_computation | async-start | bytes 524288 | tf_op jit(solution)/shard_map/psum | solution.py:73
  8.7 101.6 %copy-start.1 = (f32[1,2,64,128]{3,2,1,0:T(8,128)S(1)}, f32[1,2,64,128]{3,2,1,0:T(8,128)}, u32[]{:S(2)}) copy-start(f32[1,2,64,128]{3,2,1,0:T(8,128)} %param.5) | copy-start | bytes 196612
  72.3 93.0 %all-reduce.5.cloned.1.call-start = ((), (), s32[]{:S(2)}) async-start(), calls=%async_computation.1 | async-start | bytes 524288 | tf_op jit(solution)/shard_map/psum | solution.py:73
  108.9 1.4 collective-permute-start
Sparse Core Ops, SparseCore 0:
  9.6 56.9 all-gather.4
  72.4 34.5 all-reduce.2
  129.8 35.4 all-reduce.4
where the time goes:
time: 175 us; the launch traced here: 174 us
  waiting for transfers between devices  90.3 us (52%)
  blocking collectives  52.3 us (30%)
  matrix products  15.3 us (9%)
  between operations  13.9 us (8%)
    psum x2, waiting for transfers between devices, on_device(): summed = lax.psum(partial_front, 'rows')  69.7 us
    all_gather x2, blocking collectives, on_device(): gathered = lax.all_gather(target, 'rows', axis=1, tiled=True)  28.6 us
    all_gather x1, blocking collectives, on_device(): lax.all_gather(inverses, 'rows', axis=1, tiled=True)  23.7 us
    all_gather x1, waiting for transfers between devices, on_device(): lax.all_gather(lowers, 'rows', axis=1, tiled=True)  18.6 us
    dot_general x18, matrix products, product(): lax.dot_general(left, right, (((left.ndim - 1,), (right.ndim - 1,)), ((),...  15.3 us
  transfers between devices with their start and end apart: 4, of which 4 were waited for; matrix products, arithmetic and copies ran while one was open for 1% of the time, Pallas kernels for 0%

commit v1 on v0

--- a/solution.py
+++ b/solution.py
@@ -63,7 +63,14 @@
             pending = pending + partner(pending, "leaf", level - 1)
             target = targets[level] - pending[:, height * width :]
             pending = pending[:, : height * width]
-        gathered = lax.all_gather(target, "rows", axis=1, tiled=True)
+        ring = [target]
+        for hop in range(3):
+            ring.append(lax.ppermute(ring[-1], "rows", [(dev, (dev + 1) % 4) for dev in range(4)]))
+        gathered = jnp.roll(
+            jnp.concatenate(ring[::-1], axis=1),
+            (lax.axis_index("rows") + 1) * ring[0].shape[1],
+            axis=1,
+        )
         joined = solve_rows(
             gathered, inverse_all[level], [rows[level] for rows in prefix_rows], width
         )

time: 175 us -> 177 us (1.011)
  blocking collectives: 52.3 us -> 23.5 us
  waiting for transfers between devices: 90.3 us -> 117 us
  starting transfers between devices: 0.19 us -> 4.74 us
    all_gather x2 -> x0, blocking collectives: 28.6 us -> none  [on_device(): gathered = lax.all_gather(target, 'rows', axis=1, tiled=True)]
    ppermute x0 -> x6, waiting for transfers between devices: none -> 25.3 us  [on_device(): lax.ppermute(ring[-1], 'rows', [(dev, (dev + 1) % 4) for dev in range(4)])]
    ppermute x0 -> x6, starting transfers between devices: none -> 4.55 us  [on_device(): lax.ppermute(ring[-1], 'rows', [(dev, (dev + 1) % 4) for dev in range(4)])]
    all_gather x1, waiting for transfers between devices: 18.6 us -> 21.9 us  [on_device(): lax.all_gather(lowers, 'rows', axis=1, tiled=True)]
    psum x2, waiting for transfers between devices: 69.7 us -> 67.6 us  [on_device(): summed = lax.psum(partial_front, 'rows')]
  transfers between devices with their start and end apart: 4 -> 10, of which waited for: 4 -> 9; matrix products, arithmetic and copies ran while one was open for 1% -> 1% of each run, Pallas kernels for 0% -> 0%
where the time goes in v1:
time: 177 us
  waiting for transfers between devices  117 us (66%)
  blocking collectives  23.5 us (13%)
  matrix products  15.3 us (9%)
  between operations  13.9 us (8%)
  starting transfers between devices  4.74 us (3%)
    psum x2, waiting for transfers between devices, on_device(): summed = lax.psum(partial_front, 'rows')  67.6 us
    ppermute x6, waiting for transfers between devices, on_device(): lax.ppermute(ring[-1], 'rows', [(dev, (dev + 1) % 4) for dev in range(4)])  25.3 us
    all_gather x1, blocking collectives, on_device(): lax.all_gather(inverses, 'rows', axis=1, tiled=True)  23.5 us
    all_gather x1, waiting for transfers between devices, on_device(): lax.all_gather(lowers, 'rows', axis=1, tiled=True)  21.9 us
    dot_general x18, matrix products, product(): lax.dot_general(left, right, (((left.ndim - 1,), (right.ndim - 1,)), ((),...  15.3 us
    ppermute x6, starting transfers between devices, on_device(): lax.ppermute(ring[-1], 'rows', [(dev, (dev + 1) % 4) for dev in range(4)])  4.55 us
  transfers between devices with their start and end apart: 10, of which 9 were waited for; matrix products, arithmetic and copies ran while one was open for 1% of the time, Pallas kernels for 0%

profile of v1, /device:TPU:0, one launch (start us, length us, event | category | flops | bytes accessed | tf_op | source)
XLA Modules:
  0.0 176.6 jit_solution(13958070467230166612)
XLA Ops:
  7.2 0.7 all-gather.4.cloned.1.call-update
  8.0 0.8 slice_bitcast_fusion.28
  8.7 3.1 %collective-permute-start = (f32[64,128]{1,0:T(8,128)S(1)}, f32[64,128]{1,0:T(8,128)S(1)}, u32[]{:S(2)}, u32[]{:S(2)}) collective-permute-start(f32[64,128]{1,0:T(8,128)S(1)} %slice_bitcast_fusion.28), channel_id=1, source_target_pairs={{0,1},{1,2},{2,3},{3,0},{4,5},{5,6},{6,7},{7,4},{8,9},{9,10},{10,1... | collective-permute-start | bytes 98312 | tf_op jit(solution)/shard_map/ppermute | solution.py:68
  11.8 3.9 %collective-permute-done = f32[64,128]{1,0:T(8,128)S(1)} collective-permute-done((f32[64,128]{1,0:T(8,128)S(1)}, f32[64,128]{1,0:T(8,128)S(1)}, u32[]{:S(2)}, u32[]{:S(2)}) %collective-permute-start) | collective-permute-done | bytes 32800 | tf_op jit(solution)/shard_map/ppermute | solution.py:68
  15.7 5.7 %collective-permute-done.1 = f32[64,128]{1,0:T(8,128)S(1)} collective-permute-done((f32[64,128]{1,0:T(8,128)S(1)}, f32[64,128]{1,0:T(8,128)S(1)}, u32[]{:S(2)}, u32[]{:S(2)}) %collective-permute-start.1) | collective-permute-done | bytes 32800 | tf_op jit(solution)/shard_map/ppermute | solution.py:68
  21.4 23.5 %all-gather = f32[1,2,512,128]{3,2,1,0:T(8,128)S(1)} all-gather(f32[1,2,128,128]{3,2,1,0:T(8,128)} %param.8), channel_id=2, replica_groups=mesh['leaf'=8,'rows'=4] {'rows'}, dimensions={2}, use_global_device_ids=true | all-gather | bytes 655360 | tf_op jit(solution)/shard_map/all_gather | solution.py:50
  45.3 21.9 %all-gather.4.cloned.1.call-done = f32[1,2,512,512]{3,2,1,0:T(8,128)} async-done(((f32[1,2,128,512]{3,2,1,0:T(8,128)}), f32[1,2,512,512]{3,2,1,0:T(8,128)}) %all-gather.4.cloned.1.call-update) | async-done | bytes 2097168 | tf_op jit(solution)/shard_map/all_gather | solution.py:49
  67.1 1.1 convolution_subtract_fusion.5
  68.5 1.2 convolution_subtract_fusion.4
  69.9 1.3 convolution_subtract_fusion.3
  71.5 1.4 fusion.8
  73.0 34.3 %all-reduce.3.cloned.1.call-done = f32[64,1024]{1,0:T(8,128)} async-done(((f32[64,1024]{1,0:T(8,128)}), f32[64,1024]{1,0:T(8,128)}) %all-reduce.3.cloned.1.call-update) | async-done | bytes 262160 | tf_op jit(solution)/shard_map/psum | solution.py:80
  107.3 1.9 %fusion = f32[64,384]{1,0:T(8,128)S(1)} fusion(f32[64,1024]{1,0:T(8,128)} %all-reduce.3.cloned.1.call-done, s32[1024]{0:T(1024)S(1)} %bitcast.100, s32[384]{0:T(512)S(1)} %fusion.67), kind=kOutput, calls=%fused_computation | convolution fusion | flops 302383104 | bytes 366080 | tf_op jit(solution)/shard_map/dot_general | solution.py:16
  109.3 1.3 collective-permute-done.3
  110.6 1.5 collective-permute-start.4
  112.1 4.3 %collective-permute-done.4 = f32[64,128]{1,0:T(8,128)S(1)} collective-permute-done((f32[64,128]{1,0:T(8,128)S(1)}, f32[64,128]{1,0:T(8,128)S(1)}, u32[]{:S(2)}, u32[]{:S(2)}) %collective-permute-start.4) | collective-permute-done | bytes 32800 | tf_op jit(solution)/shard_map/ppermute | solution.py:68
  116.4 5.7 %collective-permute-done.5 = f32[64,128]{1,0:T(8,128)S(1)} collective-permute-done((f32[64,128]{1,0:T(8,128)S(1)}, f32[64,128]{1,0:T(8,128)S(1)}, u32[]{:S(2)}, u32[]{:S(2)}) %collective-permute-start.5) | collective-permute-done | bytes 32800 | tf_op jit(solution)/shard_map/ppermute | solution.py:68
  122.1 5.7 %collective-permute-done.6 = f32[64,128]{1,0:T(8,128)S(1)} collective-permute-done((f32[64,128]{1,0:T(8,128)S(1)}, f32[64,128]{1,0:T(8,128)S(1)}, u32[]{:S(2)}, u32[]{:S(2)}) %collective-permute-start.6) | collective-permute-done | bytes 32800 | tf_op jit(solution)/shard_map/ppermute | solution.py:68
  128.1 1.1 convolution_subtract_fusion.2
  129.5 1.2 convolution_subtract_fusion.1
  130.9 1.3 convolution_subtract_fusion
  132.5 1.4 fusion.6
  134.5 33.3 %all-reduce.5.cloned.1.call-done = f32[64,1024]{1,0:T(8,128)} async-done(((f32[64,1024]{1,0:T(8,128)}), f32[64,1024]{1,0:T(8,128)}) %all-reduce.5.cloned.1.call-update) | async-done | bytes 262160 | tf_op jit(solution)/shard_map/psum | solution.py:80
  167.8 1.6 fusion.38
  (36 shorter events, 3.7 us)
Async XLA Ops:
  7.2 64.3 %copy-start = (f32[1,2,1024,128]{3,2,1,0:T(8,128)S(1)}, f32[1,2,1024,128]{3,2,1,0:T(8,128)}, u32[]{:S(2)}) copy-start(f32[1,2,1024,128]{3,2,1,0:T(8,128)} %param.10) | copy-start | bytes 3145732
  7.2 65.8 %copy-start.2 = (s32[1,2,1024]{2,1,0:T(2,128)S(1)}, s32[1,2,1024]{2,1,0:T(2,128)}, u32[]{:S(2)}) copy-start(s32[1,2,1024]{2,1,0:T(2,128)} %param.11) | copy-start | bytes 24580
  7.2 60.0 %all-gather.4.cloned.1.call-start = ((), (), s32[]{:S(2)}) async-start(), calls=%async_computation.2 | async-start | bytes 2621440 | tf_op jit(solution)/shard_map/all_gather | solution.py:49
  7.9 99.4 %all-reduce.3.cloned.1.call-start = ((), (), s32[]{:S(2)}) async-start(), calls=%async_computation | async-start | bytes 524288 | tf_op jit(solution)/shard_map/psum | solution.py:80
  8.7 101.9 %copy-start.1 = (f32[1,2,64,128]{3,2,1,0:T(8,128)S(1)}, f32[1,2,64,128]{3,2,1,0:T(8,128)}, u32[]{:S(2)}) copy-start(f32[1,2,64,128]{3,2,1,0:T(8,128)} %param.7) | copy-start | bytes 196612
  8.7 7.0 %collective-permute-start = (f32[64,128]{1,0:T(8,128)S(1)}, f32[64,128]{1,0:T(8,128)S(1)}, u32[]{:S(2)}, u32[]{:S(2)}) collective-permute-start(f32[64,128]{1,0:T(8,128)S(1)} %slice_bitcast_fusion.28), channel_id=1, source_target_pairs={{0,1},{1,2},{2,3},{3,0},{4,5},{5,6},{6,7},{7,4},{8,9},{9,10},{10,1... | collective-permute-start | bytes 98312 | tf_op jit(solution)/shard_map/ppermute | solution.py:68
  15.7 5.7 %collective-permute-start.1 = (f32[64,128]{1,0:T(8,128)S(1)}, f32[64,128]{1,0:T(8,128)S(1)}, u32[]{:S(2)}, u32[]{:S(2)}) collective-permute-start(f32[64,128]{1,0:T(8,128)S(1)} %collective-permute-done), channel_id=1, source_target_pairs={{0,1},{1,2},{2,3},{3,0},{4,5},{5,6},{6,7},{7,4},{8,9},{9,10},{10,1... | collective-permute-start | bytes 98312 | tf_op jit(solution)/shard_map/ppermute | solution.py:68
  21.4 23.5 %collective-permute-start.2 = (f32[64,128]{1,0:T(8,128)S(1)}, f32[64,128]{1,0:T(8,128)S(1)}, u32[]{:S(2)}, u32[]{:S(2)}) collective-permute-start(f32[64,128]{1,0:T(8,128)S(1)} %collective-permute-done.1), channel_id=1, source_target_pairs={{0,1},{1,2},{2,3},{3,0},{4,5},{5,6},{6,7},{7,4},{8,9},{9,10},{10,1... | collective-permute-start | bytes 98312 | tf_op jit(solution)/shard_map/ppermute | solution.py:68
  72.9 94.9 %all-reduce.5.cloned.1.call-start = ((), (), s32[]{:S(2)}) async-start(), calls=%async_computation.1 | async-start | bytes 524288 | tf_op jit(solution)/shard_map/psum | solution.py:80
  109.2 1.4 collective-permute-start.3
  110.6 5.8 %collective-permute-start.4 = (f32[64,128]{1,0:T(8,128)S(1)}, f32[64,128]{1,0:T(8,128)S(1)}, u32[]{:S(2)}, u32[]{:S(2)}) collective-permute-start(f32[64,128]{1,0:T(8,128)S(1)} %slice_subtract_fusion), channel_id=1, source_target_pairs={{0,1},{1,2},{2,3},{3,0},{4,5},{5,6},{6,7},{7,4},{8,9},{9,10},{10,1... | collective-permute-start | bytes 98312 | tf_op jit(solution)/shard_map/ppermute | solution.py:68
  116.4 5.7 %collective-permute-start.5 = (f32[64,128]{1,0:T(8,128)S(1)}, f32[64,128]{1,0:T(8,128)S(1)}, u32[]{:S(2)}, u32[]{:S(2)}) collective-permute-start(f32[64,128]{1,0:T(8,128)S(1)} %collective-permute-done.4), channel_id=1, source_target_pairs={{0,1},{1,2},{2,3},{3,0},{4,5},{5,6},{6,7},{7,4},{8,9},{9,10},{10,1... | collective-permute-start | bytes 98312 | tf_op jit(solution)/shard_map/ppermute | solution.py:68
  122.1 5.7 %collective-permute-start.6 = (f32[64,128]{1,0:T(8,128)S(1)}, f32[64,128]{1,0:T(8,128)S(1)}, u32[]{:S(2)}, u32[]{:S(2)}) collective-permute-start(f32[64,128]{1,0:T(8,128)S(1)} %collective-permute-done.5), channel_id=1, source_target_pairs={{0,1},{1,2},{2,3},{3,0},{4,5},{5,6},{6,7},{7,4},{8,9},{9,10},{10,1... | collective-permute-start | bytes 98312 | tf_op jit(solution)/shard_map/ppermute | solution.py:68
Sparse Core Ops, SparseCore 0:
  9.6 57.5 all-gather.3
  73.0 34.2 all-reduce.2
  134.0 33.7 all-reduce.4

commit v2 on v0

--- a/solution.py
+++ b/solution.py
@@ -70,7 +70,7 @@
         own_block = lax.dynamic_slice_in_dim(joined, here * width, width, 1)
         solutions.append(own_block)
         partial_front = product(own_block, fronts[level])
-        summed = lax.psum(partial_front, "rows")
+        summed = jnp.sum(lax.all_gather(partial_front, "rows"), axis=0)
         positions = jnp.arange(height * width, dtype=jnp.int32)
         wanted = positions // width * (blocks * width) + here * width + positions % width
         hits = (wanted[:, None] == indices[level][None, :]).astype(jnp.float32)

time: 175 us -> 160 us (0.914)
  waiting for transfers between devices: 90.3 us -> 74.6 us
  other arithmetic: 0.72 us -> 3.34 us
  matrix products: 15.3 us -> 13.5 us
    psum x2 -> x0, waiting for transfers between devices: 69.7 us -> none  [on_device(): summed = lax.psum(partial_front, 'rows')]
    all_gather x0 -> x2, waiting for transfers between devices: none -> 53.9 us  [on_device(): summed = jnp.sum(lax.all_gather(partial_front, 'rows'), axis=0)]
    reduce_sum x0 -> x2, other arithmetic: none -> 2.62 us  [on_device(): summed = jnp.sum(lax.all_gather(partial_front, 'rows'), axis=0)]
    dot_general x18, matrix products: 15.3 us -> 13.5 us  [product(): lax.dot_general(left, right, (((left.ndim - 1,), (right.ndim - 1,)), ((),...]
where the time goes in v2:
time: 160 us; the launch traced here: 159 us
  waiting for transfers between devices  74.6 us (47%)
  blocking collectives  52.2 us (33%)
  between operations  13.9 us (9%)
  matrix products  13.5 us (8%)
  other arithmetic  3.34 us (2%)
    all_gather x2, waiting for transfers between devices, on_device(): summed = jnp.sum(lax.all_gather(partial_front, 'rows'), axis=0)  53.9 us
    all_gather x2, blocking collectives, on_device(): gathered = lax.all_gather(target, 'rows', axis=1, tiled=True)  28.5 us
    all_gather x1, blocking collectives, on_device(): lax.all_gather(inverses, 'rows', axis=1, tiled=True)  23.7 us
    all_gather x1, waiting for transfers between devices, on_device(): lax.all_gather(lowers, 'rows', axis=1, tiled=True)  18.7 us
    dot_general x18, matrix products, product(): lax.dot_general(left, right, (((left.ndim - 1,), (right.ndim - 1,)), ((),...  13.5 us
  transfers between devices with their start and end apart: 4, of which 4 were waited for; matrix products, arithmetic and copies ran while one was open for 1% of the time, Pallas kernels for 0%

profile of v2, /device:TPU:0, one launch (start us, length us, event | category | flops | bytes accessed | tf_op | source)
XLA Modules:
  0.0 159.2 jit_solution(5823509619396015481)
XLA Ops:
  7.2 0.7 all-gather.9.cloned.1.call-update
  8.0 0.8 slice.139
  8.7 15.1 %all-gather = f32[1,1,64,512]{3,2,1,0:T(8,128)S(1)} all-gather(f32[1,1,64,128]{3,2,1,0:T(8,128)S(1)} %slice.139), channel_id=2, replica_groups=mesh['leaf'=8,'rows'=4] {'rows'}, dimensions={3}, use_global_device_ids=true | all-gather | bytes 163840 | tf_op jit(solution)/shard_map/all_gather | solution.py:66
  23.8 23.7 %all-gather.1 = f32[1,2,512,128]{3,2,1,0:T(8,128)S(1)} all-gather(f32[1,2,128,128]{3,2,1,0:T(8,128)} %param.6), channel_id=3, replica_groups=mesh['leaf'=8,'rows'=4] {'rows'}, dimensions={2}, use_global_device_ids=true | all-gather | bytes 655360 | tf_op jit(solution)/shard_map/all_gather | solution.py:50
  47.8 18.7 %all-gather.9.cloned.1.call-done = f32[1,2,512,512]{3,2,1,0:T(8,128)} async-done(((f32[1,2,128,512]{3,2,1,0:T(8,128)}), f32[1,2,512,512]{3,2,1,0:T(8,128)}) %all-gather.9.cloned.1.call-update) | async-done | bytes 2097168 | tf_op jit(solution)/shard_map/all_gather | solution.py:49
  66.5 1.1 convolution_subtract_fusion.2
  67.8 1.2 convolution_subtract_fusion.1
  69.3 1.3 convolution_subtract_fusion
  70.9 1.4 fusion.8
  72.4 27.1 %all-gather.11.cloned.1.call-done = f32[256,1024]{1,0:T(8,128)} async-done(((f32[64,1024]{1,0:T(8,128)}), f32[256,1024]{1,0:T(8,128)}) %all-gather.11.cloned.1.call-update) | async-done | bytes 1048592 | tf_op jit(solution)/shard_map/all_gather | solution.py:73
  99.5 1.3 reduce_sum.18
  100.8 0.9 fusion
  101.8 1.3 collective-permute-done
  103.1 13.4 %all_gather.29 = f32[64,512]{1,0:T(8,128)S(1)} all-gather(f32[64,128]{1,0:T(8,128)S(1)} %slice_subtract_fusion.6), channel_id=1, replica_groups=mesh['leaf'=8,'rows'=4] {'rows'}, dimensions={1}, use_global_device_ids=true | all-gather | bytes 163840 | tf_op jit(solution)/shard_map/all_gather | solution.py:66
  116.7 1.1 fusion.30
  118.1 1.2 fusion.15
  119.5 1.3 fusion.14
  120.8 0.2 fusion.27
  121.1 1.4 fusion.6
  122.5 0.6 maximum_bitcast_fusion
  123.1 26.9 %all-gather.13.cloned.1.call-done = f32[256,1024]{1,0:T(8,128)} async-done(((f32[64,1024]{1,0:T(8,128)}), f32[256,1024]{1,0:T(8,128)}) %all-gather.13.cloned.1.call-update) | async-done | bytes 1048592 | tf_op jit(solution)/shard_map/all_gather | solution.py:73
  150.0 1.3 reduce_sum.19
  151.3 0.7 fusion.26
  152.0 0.6 copy.10
  (26 shorter events, 2.0 us)
Async XLA Ops:
  7.2 63.7 %copy-start = (f32[1,2,1024,128]{3,2,1,0:T(8,128)S(1)}, f32[1,2,1024,128]{3,2,1,0:T(8,128)}, u32[]{:S(2)}) copy-start(f32[1,2,1024,128]{3,2,1,0:T(8,128)} %param.8) | copy-start | bytes 3145732
  7.2 65.2 %copy-start.2 = (s32[1,2,1024]{2,1,0:T(2,128)S(1)}, s32[1,2,1024]{2,1,0:T(2,128)}, u32[]{:S(2)}) copy-start(s32[1,2,1024]{2,1,0:T(2,128)} %param.9) | copy-start | bytes 24580
  7.2 59.3 %all-gather.9.cloned.1.call-start = ((), (), s32[]{:S(2)}) async-start(), calls=%async_computation | async-start | bytes 2621440 | tf_op jit(solution)/shard_map/all_gather | solution.py:49
  7.9 91.5 %all-gather.11.cloned.1.call-start = ((), (), s32[]{:S(2)}) async-start(), calls=%async_computation.1 | async-start | bytes 1310720 | tf_op jit(solution)/shard_map/all_gather | solution.py:73
  67.8 35.3 %copy-start.1 = (f32[1,2,64,128]{3,2,1,0:T(8,128)S(1)}, f32[1,2,64,128]{3,2,1,0:T(8,128)}, u32[]{:S(2)}) copy-start(f32[1,2,64,128]{3,2,1,0:T(8,128)} %param.5) | copy-start | bytes 196612
  72.3 77.7 %all-gather.13.cloned.1.call-start = ((), (), s32[]{:S(2)}) async-start(), calls=%async_computation.2 | async-start | bytes 1310720 | tf_op jit(solution)/shard_map/all_gather | solution.py:73
  101.7 1.4 collective-permute-start
Sparse Core Ops, SparseCore 0:
  9.6 56.8 all-gather.8
  72.4 26.9 all-gather.10
  122.6 27.3 all-gather.12
